TPU v7x, 128 devices: a whole 4x4x4 slice. The times are simulated.
128 devices in a mesh: tenant: 32 (over z, x, y_lo), tp: 4 (over y_hi, core).
Axes of the slice: x: 4, y: 4 (y_hi: 2, y_lo: 2; y = y_hi * 2 + y_lo), z: 4, core: 2. Of those that a mesh axis runs over, the one named last changes fastest.
Arguments:
- src_tokens: bfloat16 [1536, 64, 1024], P('tenant'), may hold values from -64 to 64
- pair_tenant: int32 [1536], P('tenant'), may hold values from 0 to 31, as said below
- pair_length: int32 [1536], P('tenant'), may hold values from 1 to 64
- norm_gain: float32 [32, 1024], P('tenant'), may hold values from 0.1 to 1.9
- w_query: bfloat16 [32, 1024, 4096], P('tenant', None, 'tp'), may hold values from -1 to 1
- w_key: bfloat16 [32, 1024, 4096], P('tenant', None, 'tp'), may hold values from -1 to 1
- w_value: bfloat16 [32, 1024, 4096], P('tenant', None, 'tp'), may hold values from -0.1875 to 0.1875
- w_out: bfloat16 [32, 4096, 1024], P('tenant', 'tp'), may hold values from -0.09375 to 0.09375
- rel_bias: float32 [32, 32, 32], P('tenant', None, 'tp'), may hold values from -6 to 6
Outputs:
- layer_out: bfloat16 [65536, 1024], P(('tenant', 'tp'))
Inputs may be any that keep to these rules, and one draw needn't show every extreme that they name: `pair_tenant`: the pairs of one retriever shard bound for one tenant have pair_length summing to at most 64; in every draw some tenant receives exactly 64 tokens from every shard.
All inputs are finite; a program needn't handle non-finite values.
Results may differ from a plain program's by a relative error of at most 0.0065.
Values may be sent and summed in bfloat16 or wider, within the bound.
A program may use at most 128 MiB of HBM per device.

v0:
```python
import math
import jax
import jax.numpy as jnp
import numpy as np
from jax import lax
from jax.sharding import PartitionSpec as P


def in_blocks(value, dim, length):
    before, after = (value.shape[:dim], value.shape[dim + 1 :])
    return jnp.moveaxis(value.reshape(*before, length, -1, *after), dim, 0)


def summed_on_arrival(value, axis, dim):
    length = lax.axis_size(axis)
    pieces = lax.all_to_all(in_blocks(value, dim, length), axis, 0, 0, tiled=True)
    return jnp.sum(pieces.astype(jnp.float32), axis=0)


def bucket_grid(extent, buckets):
    offsets = np.arange(extent)[None, :] - np.arange(extent)[:, None]
    half_count = buckets // 2
    upward = np.where(offsets > 0, half_count, 0)
    distance = np.abs(offsets)
    exact_limit = half_count // 2
    ratio = np.maximum(distance, 1) / exact_limit
    spread_bucket = exact_limit + np.floor(
        np.log(ratio) / math.log(128.0 / exact_limit) * (half_count - exact_limit)
    ).astype(np.int32)
    spread_bucket = np.minimum(spread_bucket, half_count - 1)
    return (upward + np.where(distance < exact_limit, distance, spread_bucket)).astype(np.int32)


def rms_normed(tenant_rows, gain_row):
    values = tenant_rows.astype(jnp.float32)
    mean_square = jnp.mean(values * values, axis=-1, keepdims=True)
    return (values * lax.rsqrt(mean_square + 1e-06) * gain_row).astype(jnp.bfloat16)


def pack_rows(tokens, tenant, length, first_id, tenants):
    shard_pairs, slot_rows, feature_count = tokens.shape
    pair_order = jnp.arange(shard_pairs, dtype=jnp.int32)
    earlier = (tenant[:, None] == tenant[None, :]) & (pair_order[None, :] < pair_order[:, None])
    offset = jnp.sum(jnp.where(earlier, length[None, :], 0), axis=1)
    position = jnp.arange(slot_rows, dtype=jnp.int32)
    target = (tenant * slot_rows + offset)[:, None] + position[None, :]
    target = jnp.where(position[None, :] < length[:, None], target, tenants * slot_rows)
    flat_target = target.reshape(-1)
    packed = (
        jnp.zeros((tenants * slot_rows, feature_count), tokens.dtype)
        .at[flat_target]
        .set(tokens.reshape(-1, feature_count), mode="drop")
    )
    pair_ids = jnp.broadcast_to((first_id + pair_order)[:, None], target.shape).reshape(-1)
    segment = (
        jnp.full((tenants * slot_rows,), -1, jnp.int32).at[flat_target].set(pair_ids, mode="drop")
    )
    return (packed.reshape(tenants, slot_rows, feature_count), segment.reshape(tenants, slot_rows))


def attend(normed, segment, query_weight, key_weight, value_weight, bias_table, slot_rows, tenants):
    row_total = normed.shape[0]
    local_heads = bias_table.shape[1]
    head_size = query_weight.shape[1] // local_heads
    query_rows = jnp.dot(normed, query_weight, preferred_element_type=jnp.float32).astype(
        jnp.bfloat16
    )
    key_rows = jnp.dot(normed, key_weight, preferred_element_type=jnp.float32).astype(jnp.bfloat16)
    value_rows = jnp.dot(normed, value_weight, preferred_element_type=jnp.float32).astype(
        jnp.bfloat16
    )
    block_rows = slot_rows * min(max(1, 128 // slot_rows), tenants)
    block_count = row_total // block_rows
    bucket_index = jnp.asarray(bucket_grid(block_rows, bias_table.shape[0]))
    bucket_match = (
        bucket_index[:, :, None] == jnp.arange(bias_table.shape[0], dtype=jnp.int32)[None, None, :]
    ).astype(jnp.float32)
    position_bias = jnp.einsum(
        "qkb,bh->hqk", bucket_match, bias_table, precision=lax.Precision.HIGHEST
    )
    query_blocks = query_rows.reshape(block_count, block_rows, local_heads, head_size)
    key_blocks = key_rows.reshape(block_count, block_rows, local_heads, head_size)
    value_blocks = value_rows.reshape(block_count, block_rows, local_heads, head_size)
    scores = jnp.einsum(
        "bqhd,bkhd->bhqk", query_blocks, key_blocks, preferred_element_type=jnp.float32
    )
    scores = scores + position_bias[None]
    segment_blocks = segment.reshape(block_count, block_rows)
    allowed = (segment_blocks[:, :, None] == segment_blocks[:, None, :]) & (
        segment_blocks[:, None, :] >= 0
    )
    scores = jnp.where(allowed[:, None], scores, -1000000000.0)
    maxima = jnp.max(scores, axis=-1, keepdims=True)
    weights = jnp.exp(scores - maxima)
    probabilities = (weights / jnp.sum(weights, axis=-1, keepdims=True)).astype(jnp.bfloat16)
    context = jnp.einsum(
        "bhqk,bkhd->bqhd", probabilities, value_blocks, preferred_element_type=jnp.float32
    )
    return context.astype(jnp.bfloat16).reshape(row_total, local_heads * head_size)


def per_device(
    src_tokens, pair_tenant, pair_length, norm_gain, w_query, w_key, w_value, w_out, rel_bias
):
    tenants = lax.axis_size("tenant")
    shard_pairs, slot_rows, feature_count = src_tokens.shape
    first_id = lax.axis_index("tenant") * shard_pairs
    column_share = feature_count // lax.axis_size("tp")
    columns = lax.dynamic_slice_in_dim(
        src_tokens, lax.axis_index("tp") * column_share, column_share, 2
    )
    packed, segment = pack_rows(columns, pair_tenant, pair_length, first_id, tenants)
    arrived, arrived_segment = (
        lax.all_to_all(packed, "tenant", split_axis=0, concat_axis=0, tiled=True),
        lax.all_to_all(segment, "tenant", split_axis=0, concat_axis=0, tiled=True),
    )
    arrived = lax.all_gather(
        arrived.reshape(tenants * slot_rows, column_share), "tp", axis=1, tiled=True
    )
    arrived_segment = arrived_segment.reshape(-1)
    normed = rms_normed(arrived, norm_gain[0])
    context = attend(
        normed, arrived_segment, w_query[0], w_key[0], w_value[0], rel_bias[0], slot_rows, tenants
    )
    out_weight = w_out[0]
    row_total = arrived.shape[0]
    own_rows = row_total // lax.axis_size("tp")
    head_total = summed_on_arrival(
        jnp.dot(context, out_weight, preferred_element_type=jnp.float32).astype(jnp.bfloat16),
        "tp",
        0,
    )
    first_row = lax.axis_index("tp") * own_rows
    residual = lax.dynamic_slice_in_dim(arrived, first_row, own_rows, 0).astype(jnp.float32)
    occupied = lax.dynamic_slice_in_dim(arrived_segment, first_row, own_rows, 0) >= 0
    return jnp.where(occupied[:, None], residual + head_total, 0.0).astype(jnp.bfloat16)


def solution(mesh):
    in_specs = (
        P("tenant", None, None),
        P("tenant"),
        P("tenant"),
        P("tenant", None),
        P("tenant", None, "tp"),
        P("tenant", None, "tp"),
        P("tenant", None, "tp"),
        P("tenant", "tp", None),
        P("tenant", None, "tp"),
    )
    out_specs = P(("tenant", "tp"), None)
    return jax.shard_map(
        per_device, mesh=mesh, in_specs=in_specs, out_specs=out_specs, check_vma=False
    )
```

profile of v0, /device:TPU:1, one launch (start us, length us, event | category | flops | bytes accessed | tf_op | source)
XLA Modules:
  0.0 213.1 jit_solution(8039649190054375029)
XLA Ops:
  6.5 0.0 copy-start
  6.5 0.0 all-gather.2.cloned.1.call-start
  6.6 1.0 select_reduce_fusion
  7.6 0.7 multiply_add_fusion
  8.2 0.7 add_select_fusion.4
  9.0 0.1 select_n.47
  9.1 2.7 %constant_dynamic-slice_fusion = bf16[48,64,256]{2,1,0:T(8,128)(2,1)} fusion(bf16[48,64,1024]{2,1,0:T(8,128)(2,1)} %param.10, s32[]{:T(128)S(6)} %select_n.50), kind=kLoop, calls=%fused_computation.55 | loop fusion | bytes 3145732 | tf_op jit(solution)/shard_map/dynamic_slice | solution.py:109
  11.8 14.2 %scatter_custom_fusion.1 = bf16[2048,256]{1,0:T(8,128)(2,1)S(1)} fusion(s32[3072]{0:T(1024)S(1)} %bitcast.57, bf16[3072,256]{1,0:T(8,128)(2,1)} %bitcast.55, bf16[]{:T(256)} %constant.10.clone.1), kind=kCustom, calls=%fused_computation.40 | custom fusion | bytes 1049088 | tf_op jit(solution)/shard_map/scatter | solution.py:52
  26.0 26.3 %all_to_all.19 = bf16[32,64,256]{2,1,0:T(8,128)(2,1)} all-to-all(bf16[32,64,256]{2,1,0:T(8,128)(2,1)S(1)} %bitcast.54), channel_id=1, replica_groups=mesh['tenant'=32,'tp'=4] {'tenant'}, dimensions={0} | all-to-all | bytes 2097152 | tf_op jit(solution)/shard_map/all_to_all | solution.py:114
  52.3 0.0 all-gather.2.cloned.1.call-update
  52.4 0.1 broadcast_in_dim.78
  52.4 0.1 reshape.140
  52.5 11.8 %scatter_custom_fusion = s32[2048]{0:T(1024)S(1)} fusion(s32[3072]{0:T(1024)S(1)} %bitcast.58, s32[3072]{0:T(1024)S(1)} %reshape.140, s32[]{:T(128)} %constant.18.clone.1), kind=kCustom, calls=%fused_computation.51 | custom fusion | bytes 8196 | tf_op jit(solution)/shard_map/scatter | solution.py:56
  64.3 0.7 all_to_all.12
  65.0 4.0 %all-to-all-start = ((s32[32,1,64]{2,1,0:T(1,128)}), s32[32,1,64]{2,1,0:T(1,128)S(1)}, u32[]{:S(2)}, u32[]{:S(2)}) async-start(s32[32,1,64]{2,1,0:T(1,128)} %all_to_all.12), calls=%async_computation | async-start | bytes 32768 | tf_op jit(solution)/shard_map/all_to_all | solution.py:115
  69.1 0.7 fusion.27
  69.8 0.2 copy.30
  70.0 5.9 %all-to-all-done = s32[32,1,64]{2,1,0:T(1,128)S(1)} async-done(((s32[32,1,64]{2,1,0:T(1,128)}), s32[32,1,64]{2,1,0:T(1,128)S(1)}, u32[]{:S(2)}, u32[]{:S(2)}) %all-to-all-start) | async-done | bytes 8224 | tf_op jit(solution)/shard_map/all_to_all | solution.py:115
  75.9 0.1 eq.48
  76.0 1.3 compare_and_fusion
  77.3 13.9 %all-gather.2.cloned.1.call-done = bf16[2048,1024]{1,0:T(8,128)(2,1)} async-done(((bf16[2048,256]{1,0:T(8,128)(2,1)}), bf16[2048,1024]{1,0:T(8,128)(2,1)}) %all-gather.2.cloned.1.call-update) | async-done | bytes 4194320 | tf_op jit(solution)/shard_map/all_gather | solution.py:117
  91.3 3.2 %fusion.1 = f32[2048]{0:T(1024)S(1)} fusion(bf16[2048,1024]{1,0:T(8,128)(2,1)} %all-gather.2.cloned.1.call-done), kind=kLoop, calls=%fused_computation.5 | loop fusion | flops 6289408 | bytes 4202496 | tf_op jit(solution)/shard_map/reduce_sum | solution.py:36
  94.5 0.0 copy-done
  94.5 0.0 copy-done.9
  94.5 0.2 copy-done.2
  94.7 4.8 %convert_bitcast_fusion.2 = bf16[256,8,8,128]{3,1,2,0:T(8,128)(2,1)S(1)} fusion(bf16[1,1024,1024]{2,1,0:T(8,128)(2,1)S(1)} %copy-done, bf16[2048,1024]{1,0:T(8,128)(2,1)S(1)} %copy-done.2, f32[1024]{0:T(1024)S(1)} %bitcast.59, f32[2048]{0:T(1024)S(1)} %add_rsqrt_fusion), kind=kOutput, calls=%fused_computation.26 | convolution fusion | flops 4305453056 | bytes 10498048 | tf_op jit(solution)/shard_map/dot_general | solution.py:65
  99.6 0.0 copy-start.6
  99.6 1.1 copy.36
  100.7 0.4 copy-done.6
  101.2 4.8 %convert_bitcast_fusion.1 = bf16[256,8,8,128]{3,1,2,0:T(8,128)(2,1)S(1)} fusion(bf16[1,1024,1024]{2,1,0:T(8,128)(2,1)S(1)} %copy-done.6, bf16[2048,1024]{1,0:T(8,128)(2,1)S(1)} %copy-done.2, f32[1024]{0:T(1024)S(1)} %bitcast.60, f32[2048]{0:T(1024)S(1)} %add_rsqrt_fusion), kind=kOutput, calls=%fused_computation.25 | convolution fusion | flops 4305453056 | bytes 10498048 | tf_op jit(solution)/shard_map/dot_general | solution.py:68
  106.0 0.0 copy-start.7
  106.0 1.1 copy.37
  107.2 0.4 copy-done.7
  107.6 5.1 %convert_bitcast_fusion.3 = bf16[256,8,8,128]{3,1,2,0:T(8,128)(2,1)S(1)} fusion(bf16[1,1024,1024]{2,1,0:T(8,128)(2,1)S(1)} %copy-done.7, bf16[2048,1024]{1,0:T(8,128)(2,1)S(1)} %copy-done.2, f32[1024]{0:T(1024)S(1)} %bitcast.61, f32[2048]{0:T(1024)S(1)} %add_rsqrt_fusion), kind=kOutput, calls=%fused_computation.27 | convolution fusion | flops 4305453056 | bytes 10498048 | tf_op jit(solution)/shard_map/dot_general | solution.py:69
  112.7 3.0 %copy.35 = bf16[256,8,8,128]{3,2,1,0:T(8,128)(2,1)} copy(bf16[256,8,8,128]{3,1,2,0:T(8,128)(2,1)S(1)} %convert_bitcast_fusion.3) | data formatting | bytes 8388608
  115.7 3.0 %fusion.10 = f32[16,8,128,128]{2,3,1,0:T(8,128)S(1)} fusion(bf16[16,128,8,128]{3,2,1,0:T(8,128)(2,1)S(1)} %bitcast.49, bf16[16,128,8,128]{3,2,1,0:T(8,128)(2,1)S(1)} %bitcast.48), kind=kOutput, calls=%fused_computation.18 | convolution fusion | flops 536870912 | bytes 16777216 | tf_op jit(solution)/shard_map/bqhd,bkhd->bhqk/dot_general | solution.py:84
  118.7 4.3 %fusion.39 = (f32[16,8,128]{2,1,0:T(8,128)S(1)}, f32[16,8,128,128]{2,3,1,0:T(8,128)}) fusion(f32[16,8,128,128]{2,3,1,0:T(8,128)S(1)} %fusion.10, f32[8,128,128]{1,2,0:T(8,128)S(1)} %copy.30, pred[16,128,128]{1,2,0:T(8,128)(4,1)S(1)} %copy-done.3), kind=kOutput, calls=%fused_computation.58 | output fusion | flops 12583039 | bytes 17629184 | tf_op jit(solution)/shard_map/sub | solution.py:94
  123.0 8.2 %convert_bitcast_fusion = bf16[16,128,8,128]{1,3,2,0:T(8,128)(2,1)} fusion(f32[16,8,128,128]{2,3,1,0:T(8,128)} %get-tuple-element.6, f32[16,8,128]{2,1,0:T(8,128)S(1)} %get-tuple-element.5, bf16[16,128,8,128]{3,2,1,0:T(8,128)(2,1)} %bitcast.51), kind=kOutput, calls=%fused_computation.21 | convolution fusion | flops 543162368 | bytes 16842752 | tf_op jit(solution)/shard_map/bhqk,bkhd->bqhd/dot_general | solution.py:96
  131.3 6.9 %copy.33 = bf16[16,128,8,128]{3,2,1,0:T(8,128)(2,1)} copy(bf16[16,128,8,128]{1,3,2,0:T(8,128)(2,1)} %convert_bitcast_fusion) | data formatting | bytes 8388608 | tf_op jit(solution)/shard_map/convert_element_type | solution.py:99
  138.2 8.3 %fusion.17 = bf16[2048,1024]{1,0:T(8,128)(2,1)} fusion(bf16[256,8,8,128]{3,2,1,0:T(8,128)(2,1)} %bitcast.52, bf16[1,1024,1024]{2,1,0:T(8,128)(2,1)S(1)} %copy-done.8), kind=kOutput, calls=%fused_computation.29 | convolution fusion | flops 4297064448 | bytes 10485760 | tf_op jit(solution)/shard_map/dot_general | solution.py:129
  146.5 5.1 %all-to-all-start.2 = ((bf16[4,512,1024]{2,1,0:T(8,128)(2,1)}), bf16[4,512,1024]{2,1,0:T(8,128)(2,1)}, u32[]{:S(2)}, u32[]{:S(2)}) async-start(bf16[4,512,1024]{2,1,0:T(8,128)(2,1)} %bitcast.50), calls=%async_computation.2 | async-start | bytes 8388608 | tf_op jit(solution)/shard_map/all_to_all | solution.py:16
  151.6 0.5 broadcast.81
  152.1 0.7 reduce.5
  152.8 0.1 reshape.127
  152.9 0.1 dynamic-slice_compare_fusion
  152.9 47.4 %all-to-all-done.2 = bf16[4,512,1024]{2,1,0:T(8,128)(2,1)} async-done(((bf16[4,512,1024]{2,1,0:T(8,128)(2,1)}), bf16[4,512,1024]{2,1,0:T(8,128)(2,1)}, u32[]{:S(2)}, u32[]{:S(2)}) %all-to-all-start.2) | async-done | bytes 4194336 | tf_op jit(solution)/shard_map/all_to_all | solution.py:16
  200.4 3.4 %convert_reduce_fusion = f32[512,1024]{1,0:T(8,128)S(1)} fusion(bf16[4,512,1024]{2,1,0:T(8,128)(2,1)} %all-to-all-done.2), kind=kLoop, calls=%fused_computation.8 | loop fusion | flops 3670016 | bytes 6291456 | tf_op jit(solution)/shard_map/reduce_sum | solution.py:17
  203.8 2.5 %select_convert_fusion = bf16[512,1024]{1,0:T(8,128)(2,1)} fusion(f32[512,1024]{1,0:T(8,128)S(1)} %convert_reduce_fusion, bf16[2048,1024]{1,0:T(8,128)(2,1)} %all-gather.2.cloned.1.call-done, s32[]{:T(128)S(6)} %select_n.49, pred[512]{0:T(512)(128)(4,1)S(1)} %dynamic-slice_compare_fusion), kind=kLoop, calls=%fused_computation.34 | loop fusion | flops 2097152 | bytes 4194820 | tf_op jit(solution)/shard_map/convert_element_type | solution.py:136
  (16 shorter events, 0.1 us)
Async XLA Ops:
  6.5 88.0 %copy-start = (bf16[1,1024,1024]{2,1,0:T(8,128)(2,1)S(1)}, bf16[1,1024,1024]{2,1,0:T(8,128)(2,1)}, u32[]{:S(2)}) copy-start(bf16[1,1024,1024]{2,1,0:T(8,128)(2,1)} %param.14) | copy-start | bytes 6291460
  6.5 62.5 %copy-start.4 = (s32[128,128]{1,0:T(8,128)S(1)}, s32[128,128]{1,0:T(8,128)}, u32[]{:S(2)}) copy-start(s32[128,128]{1,0:T(8,128)} %constant.44.clone) | copy-start | bytes 196612
  6.5 62.5 %copy-start.5 = (f32[1,32,8]{1,2,0:T(8,128)S(1)}, f32[1,32,8]{1,2,0:T(8,128)}, u32[]{:S(2)}) copy-start(f32[1,32,8]{1,2,0:T(8,128)} %param.18) | copy-start | bytes 3076
  6.5 84.7 %all-gather.2.cloned.1.call-start = ((), (), s32[]{:S(2)}) async-start(), calls=%async_computation.3 | async-start | bytes 5242880 | tf_op jit(solution)/shard_map/all_gather | solution.py:117
  52.3 42.2 %copy-start.9 = (f32[1,1024]{1,0:T(1,128)S(1)}, f32[1,1024]{1,0:T(1,128)}, u32[]{:S(2)}) copy-start(f32[1,1024]{1,0:T(1,128)} %param.13) | copy-start | bytes 12292
  65.0 10.9 %all-to-all-start = ((s32[32,1,64]{2,1,0:T(1,128)}), s32[32,1,64]{2,1,0:T(1,128)S(1)}, u32[]{:S(2)}, u32[]{:S(2)}) async-start(s32[32,1,64]{2,1,0:T(1,128)} %all_to_all.12), calls=%async_computation | async-start | bytes 32768 | tf_op jit(solution)/shard_map/all_to_all | solution.py:115
  91.3 3.4 %copy-start.2 = (bf16[2048,1024]{1,0:T(8,128)(2,1)S(1)}, bf16[2048,1024]{1,0:T(8,128)(2,1)}, u32[]{:S(2)}) copy-start(bf16[2048,1024]{1,0:T(8,128)(2,1)} %all-gather.2.cloned.1.call-done) | copy-start | bytes 12582916
  99.6 1.6 copy-start.6
  106.0 1.6 copy-start.7
  115.7 3.0 %copy-start.3 = (pred[16,128,128]{1,2,0:T(8,128)(4,1)S(1)}, pred[16,128,128]{1,2,0:T(8,128)(4,1)}, u32[]{:S(2)}) copy-start(pred[16,128,128]{1,2,0:T(8,128)(4,1)} %compare_and_fusion) | copy-start | bytes 786436
  131.3 6.9 %copy-start.8 = (bf16[1,1024,1024]{2,1,0:T(8,128)(2,1)S(1)}, bf16[1,1024,1024]{2,1,0:T(8,128)(2,1)}, u32[]{:S(2)}) copy-start(bf16[1,1024,1024]{2,1,0:T(8,128)(2,1)} %param.17) | copy-start | bytes 6291460
  146.5 53.9 %all-to-all-start.2 = ((bf16[4,512,1024]{2,1,0:T(8,128)(2,1)}), bf16[4,512,1024]{2,1,0:T(8,128)(2,1)}, u32[]{:S(2)}, u32[]{:S(2)}) async-start(bf16[4,512,1024]{2,1,0:T(8,128)(2,1)} %bitcast.50), calls=%async_computation.2 | async-start | bytes 8388608 | tf_op jit(solution)/shard_map/all_to_all | solution.py:16
  152.9 53.4 %copy-start.1 = (bf16[1,1024,1024]{2,1,0:T(8,128)(2,1)S(1)}, bf16[1,1024,1024]{2,1,0:T(8,128)(2,1)}, u32[]{:S(2)}) copy-start(bf16[1,1024,1024]{2,1,0:T(8,128)(2,1)} %param.14) | copy-start | bytes 6291460
Sparse Core Ops, SparseCore 0:
  52.5 38.7 all-gather.1
where the time goes:
time: 214 us; the launch traced here: 213 us
  waiting for transfers between devices  67.2 us (31%)
  local copies, waits for them, and re-layouts  43.8 us (20%)
  matrix products  35.1 us (16%)
  blocking collectives  26.3 us (12%)
  other arithmetic  18 us (8%)
  between operations  13.6 us (6%)
  starting transfers between devices  9.12 us (4%)
    all_to_all x1, waiting for transfers between devices, summed_on_arrival(): lax.all_to_all(in_blocks(value, dim, length), axis, 0, 0, tiled=True)  47.4 us
    all_to_all x1, blocking collectives, per_device(): lax.all_to_all(packed, 'tenant', split_axis=0, concat_axis=0, tiled=True)  26.3 us
    scatter x1, local copies, waits for them, and re-layouts, pack_rows(): packed = jnp.zeros((tenants * slot_rows, feature_count), tokens.dtype).at...  14.2 us
    all_gather x1, waiting for transfers between devices, per_device(): lax.all_gather(arrived.reshape(tenants * slot_rows, column_share), 'tp',...  13.9 us
    scatter x1, local copies, waits for them, and re-layouts, pack_rows(): jnp.full((tenants * slot_rows,), -1, jnp.int32).at[flat_target]  11.8 us
    dot_general x1, matrix products, per_device(): jnp.dot(context, out_weight, preferred_element_type=jnp.float32)  8.33 us
    dot_general x1, matrix products, attend(): jnp.einsum('bhqk,bkhd->bqhd', probabilities, value_blocks, preferred_elem...  8.23 us
    convert_element_type x1, local copies, waits for them, and re-layouts, attend(): context.astype(jnp.bfloat16).reshape(row_total, local_heads * head_size)  6.88 us
  transfers between devices with their start and end apart: 3, of which 3 were waited for; matrix products, arithmetic and copies ran while one was open for 7% of the time, Pallas kernels for 0%

commit v1 on v0

--- a/solution.py
+++ b/solution.py
@@ -114,8 +114,14 @@
         lax.all_to_all(packed, "tenant", split_axis=0, concat_axis=0, tiled=True),
         lax.all_to_all(segment, "tenant", split_axis=0, concat_axis=0, tiled=True),
     )
-    arrived = lax.all_gather(
-        arrived.reshape(tenants * slot_rows, column_share), "tp", axis=1, tiled=True
+    arrived = jnp.concatenate(
+        lax.all_to_all(
+            jnp.stack([arrived.reshape(tenants * slot_rows, column_share)] * lax.axis_size("tp")),
+            "tp",
+            0,
+            0,
+        ),
+        axis=1,
     )
     arrived_segment = arrived_segment.reshape(-1)
     normed = rms_normed(arrived, norm_gain[0])

time: 214 us -> 247 us (1.15)
  waiting for transfers between devices: 67.2 us -> 88.7 us
  starting transfers between devices: 9.12 us -> 22.7 us
  between operations: 13.6 us -> 0.22 us
  local copies, waits for them, and re-layouts: 43.8 us -> 56.3 us
    all_to_all x0 -> x1, waiting for transfers between devices: none -> 45.2 us  [per_device(): lax.all_to_all(jnp.stack([arrived.reshape(tenants * slot_rows, column_sha...]
    all_gather x1 -> x0, waiting for transfers between devices: 13.9 us -> none  [per_device(): lax.all_gather(arrived.reshape(tenants * slot_rows, column_share), 'tp',...]
    all_to_all x0 -> x1, starting transfers between devices: none -> 7.27 us  [per_device(): lax.all_to_all(jnp.stack([arrived.reshape(tenants * slot_rows, column_sha...]
    all_to_all x0 -> x1, local copies, waits for them, and re-layouts: none -> 6.27 us  [per_device(): lax.all_to_all(jnp.stack([arrived.reshape(tenants * slot_rows, column_sha...]
    all_to_all x1, waiting for transfers between devices: 5.86 us -> 0.01 us  [per_device(): lax.all_to_all(segment, 'tenant', split_axis=0, concat_axis=0, tiled=True)]
    all_to_all x1, starting transfers between devices: 4.05 us -> 9.71 us  [per_device(): lax.all_to_all(segment, 'tenant', split_axis=0, concat_axis=0, tiled=True)]
    all_to_all x1, waiting for transfers between devices: 47.4 us -> 43.5 us  [summed_on_arrival(): lax.all_to_all(in_blocks(value, dim, length), axis, 0, 0, tiled=True)]
    unnamed x23 -> x25, local copies, waits for them, and re-layouts: 6.39 us -> 8.07 us
  transfers between devices with their start and end apart: 3 -> 3, of which waited for: 3 -> 2; matrix products, arithmetic and copies ran while one was open for 7% -> 10% of each run, Pallas kernels for 0% -> 0%
where the time goes in v1:
time: 247 us; the launch traced here: 246 us
  waiting for transfers between devices  88.7 us (36%)
  local copies, waits for them, and re-layouts  56.3 us (23%)
  matrix products  35.4 us (14%)
  blocking collectives  24 us (10%)
  starting transfers between devices  22.7 us (9%)
  other arithmetic  18.4 us (7%)
    all_to_all x1, waiting for transfers between devices, per_device(): lax.all_to_all(jnp.stack([arrived.reshape(tenants * slot_rows, column_sha...  45.2 us
    all_to_all x1, waiting for transfers between devices, summed_on_arrival(): lax.all_to_all(in_blocks(value, dim, length), axis, 0, 0, tiled=True)  43.5 us
    all_to_all x1, blocking collectives, per_device(): lax.all_to_all(packed, 'tenant', split_axis=0, concat_axis=0, tiled=True)  24 us
    scatter x1, local copies, waits for them, and re-layouts, pack_rows(): packed = jnp.zeros((tenants * slot_rows, feature_count), tokens.dtype).at...  14.2 us
    scatter x1, local copies, waits for them, and re-layouts, pack_rows(): jnp.full((tenants * slot_rows,), -1, jnp.int32).at[flat_target]  11.8 us
    all_to_all x1, starting transfers between devices, per_device(): lax.all_to_all(segment, 'tenant', split_axis=0, concat_axis=0, tiled=True)  9.71 us
    dot_general x1, matrix products, per_device(): jnp.dot(context, out_weight, preferred_element_type=jnp.float32)  8.33 us
    dot_general x1, matrix products, attend(): jnp.einsum('bhqk,bkhd->bqhd', probabilities, value_blocks, preferred_elem...  8.23 us
  transfers between devices with their start and end apart: 3, of which 2 were waited for; matrix products, arithmetic and copies ran while one was open for 10% of the time, Pallas kernels for 0%

profile of v1, /device:TPU:1, one launch (start us, length us, event | category | flops | bytes accessed | tf_op | source)
XLA Modules:
  0.0 245.7 jit_solution(9393710693158774374)
XLA Ops:
  0.0 1.0 select_reduce_fusion
  1.0 0.7 multiply_add_fusion
  1.7 0.7 add_select_fusion.4
  2.4 0.1 select_n.47
  2.5 0.1 broadcast_in_dim.78
  2.6 0.1 reshape.179
  2.7 11.8 %scatter_custom_fusion = s32[2048]{0:T(1024)S(1)} fusion(s32[3072]{0:T(1024)S(1)} %bitcast.69, s32[3072]{0:T(1024)S(1)} %reshape.179, s32[]{:T(128)} %constant.18.clone.1), kind=kCustom, calls=%fused_computation.51 | custom fusion | bytes 8196 | tf_op jit(solution)/shard_map/scatter | solution.py:56
  14.5 0.7 all_to_all.15
  15.2 9.7 %all-to-all-start = ((s32[32,1,64]{2,1,0:T(1,128)}), s32[32,1,64]{2,1,0:T(1,128)S(1)}, u32[]{:S(2)}, u32[]{:S(2)}) async-start(s32[32,1,64]{2,1,0:T(1,128)} %all_to_all.15), calls=%async_computation | async-start | bytes 32768 | tf_op jit(solution)/shard_map/all_to_all | solution.py:115
  24.9 2.7 %constant_dynamic-slice_fusion.1 = bf16[48,64,256]{2,1,0:T(8,128)(2,1)} fusion(bf16[48,64,1024]{2,1,0:T(8,128)(2,1)} %param.10, s32[]{:T(128)S(6)} %select_n.50), kind=kLoop, calls=%fused_computation.56 | loop fusion | bytes 3145732 | tf_op jit(solution)/shard_map/dynamic_slice | solution.py:109
  27.6 14.2 %scatter_custom_fusion.1 = bf16[2048,256]{1,0:T(8,128)(2,1)S(1)} fusion(s32[3072]{0:T(1024)S(1)} %bitcast.70, bf16[3072,256]{1,0:T(8,128)(2,1)} %bitcast.67, bf16[]{:T(256)} %constant.10.clone.1), kind=kCustom, calls=%fused_computation.40 | custom fusion | bytes 1049088 | tf_op jit(solution)/shard_map/scatter | solution.py:52
  41.8 24.0 %all_to_all.24 = bf16[32,64,256]{2,1,0:T(8,128)(2,1)S(1)} all-to-all(bf16[32,64,256]{2,1,0:T(8,128)(2,1)S(1)} %bitcast.66), channel_id=1, replica_groups=mesh['tenant'=32,'tp'=4] {'tenant'}, dimensions={0} | all-to-all | bytes 2097152 | tf_op jit(solution)/shard_map/all_to_all | solution.py:114
  65.8 2.2 stack.3
  68.1 7.3 %all-to-all-start.2 = ((bf16[4,2048,256]{2,1,0:T(8,128)(2,1)}), bf16[4,2048,256]{2,1,0:T(8,128)(2,1)}, u32[]{:S(2)}, u32[]{:S(2)}) async-start(bf16[4,2048,256]{2,1,0:T(8,128)(2,1)} %stack.3), calls=%async_computation.2 | async-start | bytes 8388608 | tf_op jit(solution)/shard_map/all_to_all | solution.py:118
  75.3 0.5 broadcast.103
  75.9 0.7 reduce.9
  76.6 0.7 fusion.27
  77.3 0.2 copy.48
  77.5 0.1 eq.48
  77.6 1.4 compare_and_fusion
  79.0 45.2 %all-to-all-done.2 = bf16[4,2048,256]{2,1,0:T(8,128)(2,1)} async-done(((bf16[4,2048,256]{2,1,0:T(8,128)(2,1)}), bf16[4,2048,256]{2,1,0:T(8,128)(2,1)}, u32[]{:S(2)}, u32[]{:S(2)}) %all-to-all-start.2) | async-done | bytes 4194336 | tf_op jit(solution)/shard_map/all_to_all | solution.py:118
  124.1 6.3 %copy.44 = bf16[4,2048,256]{1,2,0:T(8,128)(2,1)} copy(bf16[4,2048,256]{2,1,0:T(8,128)(2,1)} %all-to-all-done.2) | data formatting | bytes 8388608 | tf_op jit(solution)/shard_map/all_to_all | solution.py:118
  130.4 3.2 %fusion.1 = f32[2048]{0:T(1024)S(1)} fusion(bf16[4,2048,256]{1,2,0:T(8,128)(2,1)} %copy.44), kind=kLoop, calls=%fused_computation.5 | loop fusion | flops 6289408 | bytes 4202496 | tf_op jit(solution)/shard_map/reduce_sum | solution.py:36
  133.6 0.2 copy-done.2
  133.8 1.0 fusion.3
  134.8 5.0 %convert_bitcast_fusion.1 = bf16[256,8,8,128]{3,1,2,0:T(8,128)(2,1)S(1)} fusion(bf16[2048,1024]{0,1:T(8,128)(2,1)S(1)} %bitcast.62, bf16[1,1024,1024]{2,1,0:T(8,128)(2,1)S(1)} %copy-done), kind=kOutput, calls=%fused_computation.25 | convolution fusion | flops 4297064448 | bytes 10485760 | tf_op jit(solution)/shard_map/dot_general | solution.py:68
  139.8 1.1 copy.56
  141.0 0.4 copy-done.7
  141.4 4.9 %convert_bitcast_fusion.2 = bf16[256,8,8,128]{3,1,2,0:T(8,128)(2,1)S(1)} fusion(bf16[2048,1024]{0,1:T(8,128)(2,1)S(1)} %bitcast.63, bf16[1,1024,1024]{2,1,0:T(8,128)(2,1)S(1)} %copy-done.7), kind=kOutput, calls=%fused_computation.26 | convolution fusion | flops 4297064448 | bytes 10485760 | tf_op jit(solution)/shard_map/dot_general | solution.py:65
  146.4 5.1 %convert_bitcast_fusion.3 = bf16[256,8,8,128]{3,1,2,0:T(8,128)(2,1)S(1)} fusion(bf16[2048,1024]{0,1:T(8,128)(2,1)S(1)} %bitcast.64, bf16[1,1024,1024]{2,1,0:T(8,128)(2,1)S(1)} %copy-done.8), kind=kOutput, calls=%fused_computation.27 | convolution fusion | flops 4297064448 | bytes 10485760 | tf_op jit(solution)/shard_map/dot_general | solution.py:69
  151.5 3.0 %copy.54 = bf16[256,8,8,128]{3,2,1,0:T(8,128)(2,1)} copy(bf16[256,8,8,128]{3,1,2,0:T(8,128)(2,1)S(1)} %convert_bitcast_fusion.3) | data formatting | bytes 8388608
  154.5 1.1 copy.55
  155.6 0.0 copy-start.3
  155.6 3.0 %fusion.10 = f32[16,8,128,128]{2,3,1,0:T(8,128)S(1)} fusion(bf16[16,128,8,128]{3,2,1,0:T(8,128)(2,1)S(1)} %bitcast.57, bf16[16,128,8,128]{3,2,1,0:T(8,128)(2,1)S(1)} %bitcast.58), kind=kOutput, calls=%fused_computation.18 | convolution fusion | flops 536870912 | bytes 16777216 | tf_op jit(solution)/shard_map/bqhd,bkhd->bhqk/dot_general | solution.py:84
  158.7 4.3 %fusion.36 = (f32[16,8,128]{2,1,0:T(8,128)S(1)}, f32[16,8,128,128]{2,3,1,0:T(8,128)}) fusion(f32[16,8,128,128]{2,3,1,0:T(8,128)S(1)} %fusion.10, f32[8,128,128]{1,2,0:T(8,128)S(1)} %copy.48, pred[16,128,128]{1,2,0:T(8,128)(4,1)S(1)} %copy-done.3), kind=kOutput, calls=%fused_computation.59 | output fusion | flops 12583039 | bytes 17629184 | tf_op jit(solution)/shard_map/sub | solution.py:94
  163.0 8.2 %convert_bitcast_fusion = bf16[16,128,8,128]{1,3,2,0:T(8,128)(2,1)} fusion(f32[16,8,128,128]{2,3,1,0:T(8,128)} %get-tuple-element.6, f32[16,8,128]{2,1,0:T(8,128)S(1)} %get-tuple-element.5, bf16[16,128,8,128]{3,2,1,0:T(8,128)(2,1)} %bitcast.61), kind=kOutput, calls=%fused_computation.21 | convolution fusion | flops 543162368 | bytes 16842752 | tf_op jit(solution)/shard_map/bhqk,bkhd->bqhd/dot_general | solution.py:96
  171.2 6.9 %copy.51 = bf16[16,128,8,128]{3,2,1,0:T(8,128)(2,1)} copy(bf16[16,128,8,128]{1,3,2,0:T(8,128)(2,1)} %convert_bitcast_fusion) | data formatting | bytes 8388608 | tf_op jit(solution)/shard_map/convert_element_type | solution.py:99
  178.1 8.3 %fusion.17 = bf16[2048,1024]{1,0:T(8,128)(2,1)} fusion(bf16[256,8,8,128]{3,2,1,0:T(8,128)(2,1)} %bitcast.65, bf16[1,1024,1024]{2,1,0:T(8,128)(2,1)S(1)} %copy-done.9), kind=kOutput, calls=%fused_computation.29 | convolution fusion | flops 4297064448 | bytes 10485760 | tf_op jit(solution)/shard_map/dot_general | solution.py:135
  186.4 5.8 %all-to-all-start.3 = ((bf16[4,512,1024]{2,1,0:T(8,128)(2,1)}), bf16[4,512,1024]{2,1,0:T(8,128)(2,1)}, u32[]{:S(2)}, u32[]{:S(2)}) async-start(bf16[4,512,1024]{2,1,0:T(8,128)(2,1)} %bitcast.60), calls=%async_computation.3 | async-start | bytes 8388608 | tf_op jit(solution)/shard_map/all_to_all | solution.py:16
  192.2 0.5 broadcast.104
  192.7 0.7 reduce.10
  193.4 0.1 reshape.165
  193.5 0.1 dynamic-slice_compare_fusion
  193.6 2.3 constant_dynamic-slice_fusion
  195.8 1.6 copy.53
  197.5 43.5 %all-to-all-done.3 = bf16[4,512,1024]{2,1,0:T(8,128)(2,1)} async-done(((bf16[4,512,1024]{2,1,0:T(8,128)(2,1)}), bf16[4,512,1024]{2,1,0:T(8,128)(2,1)}, u32[]{:S(2)}, u32[]{:S(2)}) %all-to-all-start.3) | async-done | bytes 4194336 | tf_op jit(solution)/shard_map/all_to_all | solution.py:16
  241.0 3.4 %convert_reduce_fusion = f32[512,1024]{1,0:T(8,128)S(1)} fusion(bf16[4,512,1024]{2,1,0:T(8,128)(2,1)} %all-to-all-done.3), kind=kLoop, calls=%fused_computation.8 | loop fusion | flops 3670016 | bytes 6291456 | tf_op jit(solution)/shard_map/reduce_sum | solution.py:17
  244.4 1.3 select_convert_fusion
  (23 shorter events, 0.1 us)
Async XLA Ops:
  0.0 134.8 %copy-start = (bf16[1,1024,1024]{2,1,0:T(8,128)(2,1)S(1)}, bf16[1,1024,1024]{2,1,0:T(8,128)(2,1)}, u32[]{:S(2)}) copy-start(bf16[1,1024,1024]{2,1,0:T(8,128)(2,1)} %param.15) | copy-start | bytes 6291460
  15.2 26.7 %all-to-all-start = ((s32[32,1,64]{2,1,0:T(1,128)}), s32[32,1,64]{2,1,0:T(1,128)S(1)}, u32[]{:S(2)}, u32[]{:S(2)}) async-start(s32[32,1,64]{2,1,0:T(1,128)} %all_to_all.15), calls=%async_computation | async-start | bytes 32768 | tf_op jit(solution)/shard_map/all_to_all | solution.py:115
  68.1 7.8 %copy-start.6 = (f32[1,1024]{1,0:T(1,128)S(1)}, f32[1,1024]{1,0:T(1,128)}, u32[]{:S(2)}) copy-start(f32[1,1024]{1,0:T(1,128)} %param.13) | copy-start | bytes 12292
  68.1 8.5 %copy-start.4 = (s32[128,128]{1,0:T(8,128)S(1)}, s32[128,128]{1,0:T(8,128)}, u32[]{:S(2)}) copy-start(s32[128,128]{1,0:T(8,128)} %constant.44.clone) | copy-start | bytes 196612
  68.1 8.5 %copy-start.5 = (f32[1,32,8]{1,2,0:T(8,128)S(1)}, f32[1,32,8]{1,2,0:T(8,128)}, u32[]{:S(2)}) copy-start(f32[1,32,8]{1,2,0:T(8,128)} %param.18) | copy-start | bytes 3076
  68.1 56.1 %all-to-all-start.2 = ((bf16[4,2048,256]{2,1,0:T(8,128)(2,1)}), bf16[4,2048,256]{2,1,0:T(8,128)(2,1)}, u32[]{:S(2)}, u32[]{:S(2)}) async-start(bf16[4,2048,256]{2,1,0:T(8,128)(2,1)} %stack.3), calls=%async_computation.2 | async-start | bytes 8388608 | tf_op jit(solution)/shard_map/all_to_all | solution.py:118
  130.4 3.4 %copy-start.2 = (bf16[4,2048,256]{1,2,0:T(8,128)(2,1)S(1)}, bf16[4,2048,256]{1,2,0:T(8,128)(2,1)}, u32[]{:S(2)}) copy-start(bf16[4,2048,256]{1,2,0:T(8,128)(2,1)} %copy.44) | copy-start | bytes 12582916
  139.8 1.6 copy-start.7
  141.4 5.0 %copy-start.8 = (bf16[1,1024,1024]{2,1,0:T(8,128)(2,1)S(1)}, bf16[1,1024,1024]{2,1,0:T(8,128)(2,1)}, u32[]{:S(2)}) copy-start(bf16[1,1024,1024]{2,1,0:T(8,128)(2,1)} %param.16) | copy-start | bytes 6291460
  155.6 3.1 %copy-start.3 = (pred[16,128,128]{1,2,0:T(8,128)(4,1)S(1)}, pred[16,128,128]{1,2,0:T(8,128)(4,1)}, u32[]{:S(2)}) copy-start(pred[16,128,128]{1,2,0:T(8,128)(4,1)} %compare_and_fusion) | copy-start | bytes 786436
  171.2 6.9 %copy-start.9 = (bf16[1,1024,1024]{2,1,0:T(8,128)(2,1)S(1)}, bf16[1,1024,1024]{2,1,0:T(8,128)(2,1)}, u32[]{:S(2)}) copy-start(bf16[1,1024,1024]{2,1,0:T(8,128)(2,1)} %param.17) | copy-start | bytes 6291460
  186.4 54.6 %all-to-all-start.3 = ((bf16[4,512,1024]{2,1,0:T(8,128)(2,1)}), bf16[4,512,1024]{2,1,0:T(8,128)(2,1)}, u32[]{:S(2)}, u32[]{:S(2)}) async-start(bf16[4,512,1024]{2,1,0:T(8,128)(2,1)} %bitcast.60), calls=%async_computation.3 | async-start | bytes 8388608 | tf_op jit(solution)/shard_map/all_to_all | solution.py:16
  195.8 49.9 %copy-start.1 = (bf16[1,1024,1024]{2,1,0:T(8,128)(2,1)S(1)}, bf16[1,1024,1024]{2,1,0:T(8,128)(2,1)}, u32[]{:S(2)}) copy-start(bf16[1,1024,1024]{2,1,0:T(8,128)(2,1)} %param.15) | copy-start | bytes 6291460
